TPU v7x, 32 devices: a whole 2x2x4 slice. The times are simulated.
32 devices in a mesh: wide: 16 (over z, y, core), narrow: 2 (over x).
Axes of the slice: x: 2, y: 2, z: 4, core: 2. Of those that a mesh axis runs over, the one named last changes fastest.
Arguments:
- query_coords: float32 [3, 32, 16, 32], P(None, ('wide', 'narrow')), may hold values from -1 to 1
- owner_element: int32 [32, 16, 32], P(('wide', 'narrow')), may hold values from 0 to 15
- pair_counts: int32 [32, 32], P(('wide', 'narrow')), may hold values from 0 to 16, as said below
- fields: bfloat16 [512, 8, 1024], P(('wide', 'narrow')), may hold values from -6 to 6
Outputs:
- values: bfloat16 [16, 32, 16, 32], P(None, ('wide', 'narrow'))
Inputs may be any that keep to these rules, and one draw needn't show every extreme that they name: `pair_counts`: every count is at most 16, and some pair of devices reaches 16 in every draw.
All inputs are finite; a program needn't handle non-finite values.
Results may differ from a plain program's by a relative error of at most 0.0043.
Values may be sent and summed in bfloat16 or wider, within the bound.
A program may use at most 64 MiB of HBM per device.

v0:
```python
import math

import jax
import jax.numpy as jnp
from jax import lax
from jax.sharding import PartitionSpec as P

GLL_NODES = (
    -1.0,
    -0.8717401485096066,
    -0.5917001814331423,
    -0.2092992179024789,
    0.2092992179024789,
    0.5917001814331423,
    0.8717401485096066,
    1.0,
)


def for_sending(shard):
    return jax.tree.map(lambda a: a.astype(jnp.bfloat16) if a.dtype == jnp.float32 else a, shard)


def lagrange(position):
    result = []
    for i in range(8):
        factor = jnp.ones_like(position)
        for m in range(8):
            if m != i:
                factor = factor * ((position - GLL_NODES[m]) / (GLL_NODES[i] - GLL_NODES[m]))
        result.append(factor)
    return jnp.stack(result)


def interpolate(payload, field_table):
    element_count = field_table.shape[0] // 8
    column_count = field_table.shape[1]
    half_cols = column_count // 2
    basis_r = lagrange(payload[0]).astype(jnp.bfloat16)
    tensor_st = (lagrange(payload[1])[:, None, :] * lagrange(payload[2])[None, :, :]).reshape(
        64, -1
    )
    picked = payload[3][None, :] == jnp.arange(element_count, dtype=jnp.float32)[:, None]
    weights = jnp.where(
        picked[:, None, :], basis_r[None, :, :], jnp.zeros((), jnp.bfloat16)
    ).reshape(element_count * 8, -1)
    halves = []
    for h in range(2):
        partial_value = lax.dot_general(
            field_table[:, h * half_cols : (h + 1) * half_cols],
            weights,
            (((0,), (0,)), ((), ())),
            preferred_element_type=jnp.float32,
        )
        halves.append(
            jnp.sum(partial_value.reshape(half_cols // 64, 64, -1) * tensor_st[None, :, :], axis=1)
        )
    return jnp.concatenate(halves, axis=0).astype(jnp.bfloat16)


def evaluate(payload, field_table):
    field_count = field_table.shape[1] // 64
    lead_shape = payload.shape[1:]
    flat = payload.reshape(4, -1)
    total_rows = flat.shape[1]
    block_rows = math.gcd(total_rows, 512)
    blocks = jnp.transpose(flat.reshape(4, total_rows // block_rows, block_rows), (1, 0, 2))

    def one_block(block):
        return interpolate(block, field_table)

    results = lax.map(one_block, blocks)
    return jnp.transpose(results, (1, 0, 2)).reshape((field_count,) + lead_shape)


def on_device(query_coords, owner_element, pair_counts, fields):
    wide_size = lax.axis_size("wide")
    narrow_size = lax.axis_size("narrow")
    device_count = wide_size * narrow_size
    slot_count = owner_element.shape[1]
    element_count = fields.shape[0]
    field_table = fields.reshape(element_count * fields.shape[1], fields.shape[2])
    live = jnp.arange(slot_count, dtype=jnp.int32)[:, None] < pair_counts[0][None, :]
    element_float = jnp.where(live, owner_element[0], element_count).astype(jnp.float32)
    payload = jnp.concatenate([query_coords[:, 0], element_float[None]], axis=0)
    payload = payload.reshape(4, slot_count, wide_size, narrow_size)
    arrived = lax.all_to_all(
        lax.all_to_all(payload, "wide", split_axis=2, concat_axis=2, tiled=True),
        "narrow",
        split_axis=3,
        concat_axis=3,
        tiled=True,
    )
    result = evaluate(arrived, field_table)
    returned = lax.all_to_all(
        lax.all_to_all(for_sending(result), "wide", split_axis=2, concat_axis=2, tiled=True),
        "narrow",
        split_axis=3,
        concat_axis=3,
        tiled=True,
    ).astype(result.dtype)
    return returned.reshape(returned.shape[0], 1, slot_count, device_count)


def solution(mesh):
    placed = (
        P(None, ("wide", "narrow"), None, None),
        P(("wide", "narrow"), None, None),
        P(("wide", "narrow"), None),
        P(("wide", "narrow"), None, None),
    )
    return jax.shard_map(
        on_device,
        mesh=mesh,
        in_specs=placed,
        out_specs=P(None, ("wide", "narrow"), None, None),
        check_vma=False,
    )
```

profile of v0, /device:TPU:0, one launch (start us, length us, event | category | flops | bytes accessed | tf_op | source)
XLA Modules:
  0.0 51.5 jit_solution(9558058476863743550)
XLA Ops:
  0.0 0.8 %copy.35 = s32[1,16,32]{1,2,0:T(8,128)S(1)} copy(s32[1,16,32]{2,1,0:T(8,128)} %param.5) | data formatting | bytes 4096 | tf_op args[1]
  0.9 0.7 %copy-done.2 = s32[1,32]{1,0:T(1,128)S(1)} copy-done((s32[1,32]{1,0:T(1,128)S(1)}, s32[1,32]{1,0:T(1,128)}, u32[]{:S(2)}) %copy-start.2) | copy-done | bytes 152
  1.8 13.7 %all_to_all.20 = f32[16,1,128]{2,1,0:T(1,128)S(1)} all-to-all(f32[16,1,128]{2,1,0:T(1,128)S(1)} %reshape.2410), channel_id=1, replica_groups=mesh['wide'=16,'narrow'=2] {'wide'}, dimensions={0} | all-to-all | bytes 16384 | tf_op jit(solution)/shard_map/all_to_all | solution.py:88
  15.4 0.5 broadcast.3145
  15.9 0.7 %reduce = f32[16,128]{1,0:T(8,128)S(1)} reduce(f32[16,1,128]{2,1,0:T(1,128)S(1)} %all_to_all.20, f32[]{:T(128)} %broadcast.3145), dimensions={1}, to_apply=%all_to_all.12.reduce_sub_computation | reduce | bytes 16388 | tf_op jit(solution)/shard_map/all_to_all | solution.py:88
  16.9 6.4 %all_to_all.21 = f32[2,1,1024]{2,1,0:T(1,128)S(1)} all-to-all(f32[2,1,1024]{2,1,0:T(1,128)S(1)} %reshape.2412), channel_id=1, replica_groups=mesh['wide'=16,'narrow'=2] {'narrow'}, dimensions={0} | all-to-all | bytes 16384 | tf_op jit(solution)/shard_map/all_to_all | solution.py:87
  23.2 0.7 %reduce.1 = f32[2,1024]{1,0:T(2,128)S(1)} reduce(f32[2,1,1024]{2,1,0:T(1,128)S(1)} %all_to_all.21, f32[]{:T(128)} %broadcast.3145), dimensions={1}, to_apply=%all_to_all.13.reduce_sub_computation | reduce | bytes 16388 | tf_op jit(solution)/shard_map/all_to_all | solution.py:87
  24.1 0.2 multiply_convert_fusion
  24.2 0.2 copy.38
  24.6 0.2 copy.57
  24.9 0.2 copy.55
  25.1 0.1 reshape.2394
  25.2 0.2 copy.56
  25.4 0.1 reshape.2395
  25.5 0.2 copy.62
  25.7 0.1 reshape.2401
  25.9 0.2 copy.54
  26.0 0.1 reshape.2393
  26.2 0.2 copy.46
  26.4 0.1 reshape.2409
  26.5 0.2 copy.45
  26.7 0.1 reshape.2408
  26.9 0.2 copy.44
  27.1 0.1 reshape.2407
  27.2 0.2 copy.43
  27.4 0.1 reshape.2406
  27.6 0.2 copy.42
  27.8 0.1 reshape.2405
  27.9 0.2 copy.41
  28.1 0.1 reshape.2404
  28.3 0.2 copy.39
  28.5 0.1 reshape.2402
  28.7 0.2 copy.40
  28.9 0.1 reshape.2403
  29.0 0.2 copy.53
  29.2 0.1 reshape.2392
  29.3 0.2 copy.52
  29.5 0.1 reshape.2391
  29.7 0.2 copy.51
  29.8 0.1 reshape.2390
  30.0 0.2 copy.50
  30.2 0.1 reshape.2389
  30.3 0.2 copy.49
  30.6 0.2 copy.47
  31.0 0.2 copy.48
  31.1 0.1 reshape.2387
  31.3 0.2 copy.61
  31.5 0.1 reshape.2400
  31.6 0.2 copy.60
  31.8 0.1 reshape.2399
  31.9 0.2 copy.59
  32.3 0.2 copy.58
  32.7 0.5 copy-done
  33.2 0.3 fusion
  33.5 0.4 multiply_reduce_fusion.1
  33.9 0.2 copy.63
  34.1 0.2 copy.64
  34.2 0.4 copy_bitcast_fusion.1
  34.6 0.2 reshape.2414
  34.8 9.1 %all_to_all.22 = bf16[16,2,256]{2,1,0:T(2,128)(2,1)S(1)} all-to-all(bf16[16,2,256]{2,1,0:T(2,128)(2,1)S(1)} %reshape.2414), channel_id=1, replica_groups=mesh['wide'=16,'narrow'=2] {'wide'}, dimensions={0} | all-to-all | bytes 32768 | tf_op jit(solution)/shard_map/all_to_all | solution.py:96
  44.0 0.2 reshape.2416
  44.2 6.2 %all_to_all.23 = bf16[2,2,2048]{2,1,0:T(2,128)(2,1)S(1)} all-to-all(bf16[2,2,2048]{2,1,0:T(2,128)(2,1)S(1)} %reshape.2416), channel_id=1, replica_groups=mesh['wide'=16,'narrow'=2] {'narrow'}, dimensions={0} | all-to-all | bytes 32768 | tf_op jit(solution)/shard_map/all_to_all | solution.py:95
  50.6 0.2 copy.67
  50.7 0.8 %copy.68 = bf16[16,1,16,32]{3,2,1,0:T(8,128)(2,1)} copy(bf16[16,1,16,32]{2,0,3,1:T(8,128)(2,1)S(1)} %bitcast.93) | data formatting | bytes 32768 | tf_op jit(solution)/shard_map/reshape | solution.py:102
  (27 shorter events, 2.0 us)
Async XLA Ops:
  0.0 0.8 %copy-start.1 = (f32[3,1,16,32]{3,2,1,0:T(8,128)S(1)}, f32[3,1,16,32]{3,2,1,0:T(8,128)}, u32[]{:S(2)}) copy-start(f32[3,1,16,32]{3,2,1,0:T(8,128)} %param.4) | copy-start | bytes 18436
  0.9 0.7 %copy-start.2 = (s32[1,32]{1,0:T(1,128)S(1)}, s32[1,32]{1,0:T(1,128)}, u32[]{:S(2)}) copy-start(s32[1,32]{1,0:T(1,128)} %param.6) | copy-start | bytes 388
  32.3 1.0 %copy-start = (bf16[16,8,1024]{2,1,0:T(8,128)(2,1)S(1)}, bf16[16,8,1024]{2,1,0:T(8,128)(2,1)}, u32[]{:S(2)}) copy-start(bf16[16,8,1024]{2,1,0:T(8,128)(2,1)} %param.7) | copy-start | bytes 786436
where the time goes:
time: 51.9 us; the launch traced here: 51.5 us
  blocking collectives  35.3 us (68%)
  local copies, waits for them, and re-layouts  13.2 us (25%)
  other arithmetic  2.05 us (4%)
  matrix products  0.69 us (1%)
    all_to_all x1, blocking collectives, on_device(): lax.all_to_all(payload, 'wide', split_axis=2, concat_axis=2, tiled=True)  13.7 us
    all_to_all x1, blocking collectives, on_device(): lax.all_to_all(for_sending(result), 'wide', split_axis=2, concat_axis=2,...  9.07 us
    all_to_all x1, blocking collectives, on_device(): lax.all_to_all(lax.all_to_all(payload, 'wide', split_axis=2, concat_axis=...  6.37 us
    all_to_all x1, blocking collectives, on_device(): lax.all_to_all(lax.all_to_all(for_sending(result), 'wide', split_axis=2,...  6.2 us
    mul x32, local copies, waits for them, and re-layouts, lagrange(): factor * ((position - GLL_NODES[m]) / (GLL_NODES[i] - GLL_NODES[m]))  5.1 us
    another operation x18, local copies, waits for them, and re-layouts  3.09 us
    unnamed x16, local copies, waits for them, and re-layouts  3.02 us

commit v1 on v0

v1 whole, which is shorter than its diff:
```python
import functools
import math

import jax
import jax.numpy as jnp
from jax import lax
from jax.experimental import pallas as pl
from jax.experimental.pallas import tpu as pltpu
from jax.sharding import PartitionSpec as P

GLL_NODES = (
    -1.0,
    -0.8717401485096066,
    -0.5917001814331423,
    -0.2092992179024789,
    0.2092992179024789,
    0.5917001814331423,
    0.8717401485096066,
    1.0,
)
NODE = len(GLL_NODES)
SCALES = tuple(
    1.0 / math.prod(GLL_NODES[i] - GLL_NODES[m] for m in range(NODE) if m != i)
    for i in range(NODE)
)
LANES = 128
MESH = pl.DeviceIdType.MESH


def lagrange_rows(row, node_index, scale):
    position = jnp.broadcast_to(row, (NODE, row.shape[1]))
    factors = [
        jnp.where(node_index == m, 1.0, position - GLL_NODES[m]) for m in range(NODE)
    ]
    while len(factors) > 1:
        factors = [a * b for a, b in zip(factors[::2], factors[1::2])]
    return factors[0] * scale


def kernel(
    sizes,
    coords_hbm,
    element_hbm,
    counts_hbm,
    fields_hbm,
    out_ref,
    coords,
    element,
    counts,
    fields,
    fields_t,
    send_query,
    recv_query,
    send_value,
    recv_value,
    local_sems,
    sems,
):
    wide_size, narrow_size, slots, elements, field_count = sizes
    n = wide_size * narrow_size
    width = min(n, LANES)
    packed = LANES // width
    groups = slots // packed
    me = lax.axis_index("wide") * narrow_size + lax.axis_index("narrow")

    def partner(step):
        offset = n // 2 + (1 - 2 * (step % 2)) * ((step + 1) // 2)
        index = lax.rem(me + offset, n)
        return index, (index // narrow_size, lax.rem(index, narrow_size))

    def for_partners(body):
        if n <= 64:
            for step in range(n - 1):
                body(step)
        else:
            lax.fori_loop(0, n - 1, lambda step, c: (body(step), c)[1], 0)

    loads = [
        pltpu.make_async_copy(src, dst, local_sems.at[i])
        for i, (src, dst) in enumerate(
            (
                (coords_hbm, coords),
                (element_hbm, element),
                (counts_hbm, counts),
                (fields_hbm, fields),
            )
        )
    ]
    for load in loads:
        load.start()
    barrier = pltpu.get_barrier_semaphore()

    def greet(step):
        pl.semaphore_signal(
            barrier, inc=1, device_id=partner(step)[1], device_id_type=MESH
        )

    for_partners(greet)

    for load in loads[:3]:
        load.wait()
    slot_index = lax.broadcasted_iota(jnp.int32, (slots, n), 0)
    picked = jnp.where(slot_index < counts[...], element[...], elements).astype(
        jnp.float32
    )
    pieces = []
    for k in range(packed):
        rows = slice(k * groups, (k + 1) * groups)
        pieces += [coords[0, rows], coords[1, rows], coords[2, rows], picked[rows]]
    payload = jnp.concatenate(pieces, axis=0)
    payload = jnp.concatenate(
        [payload, jnp.zeros((LANES - payload.shape[0], n), jnp.float32)], axis=0
    )
    if n < LANES:
        payload = jnp.concatenate(
            [payload, jnp.zeros((LANES, LANES - n), jnp.float32)], axis=1
        )
    send_query[0] = jnp.transpose(payload)[:n]

    pl.semaphore_wait(barrier, n - 1)

    def exchange(source, target, send_sem, recv_sem, own_sem):
        def send(step):
            index, device = partner(step)
            pltpu.make_async_remote_copy(
                src_ref=source.at[:, pl.ds(index, 1)],
                dst_ref=target.at[:, pl.ds(me, 1)],
                send_sem=send_sem,
                recv_sem=recv_sem,
                device_id=device,
                device_id_type=MESH,
            ).start()

        for_partners(send)
        pltpu.make_async_copy(
            source.at[:, pl.ds(me, 1)], target.at[:, pl.ds(me, 1)], own_sem
        ).start()

    def finish(source, target, recv_sem, own_sem):
        rest = pl.ds(0, n - 1)
        pltpu.make_async_copy(
            source.at[:, rest], target.at[:, rest], recv_sem
        ).wait()
        pltpu.make_async_copy(
            source.at[:, pl.ds(me, 1)], target.at[:, pl.ds(me, 1)], own_sem
        ).wait()

    exchange(send_query, recv_query, sems.at[0], sems.at[1], sems.at[2])

    loads[3].wait()
    fields_t[...] = jnp.transpose(
        fields[...].reshape(elements * NODE, fields.shape[2])
    )
    node_index = lax.broadcasted_iota(jnp.int32, (NODE, LANES), 0)
    scale = jnp.zeros((NODE, LANES), jnp.float32)
    for i in range(NODE):
        scale = jnp.where(node_index == i, jnp.float32(SCALES[i]), scale)

    finish(send_query, recv_query, sems.at[1], sems.at[2])

    def evaluate(block):
        rows = pl.ds(block * width, width)
        arrived = recv_query[0, rows]
        if width < LANES:
            arrived = jnp.concatenate(
                [arrived, jnp.zeros((LANES - width, LANES), jnp.float32)], axis=0
            )
        turned = jnp.transpose(arrived)[:, :width]
        span = 4 * groups
        queries = jnp.concatenate(
            [turned[k * span : (k + 1) * span] for k in range(packed)], axis=1
        )
        results = []
        for g in range(groups):
            r, s, t, e = (queries[c * groups + g :][:1] for c in range(4))
            basis_r = lagrange_rows(r, node_index, scale)
            basis_s = lagrange_rows(s, node_index, scale)
            basis_t = lagrange_rows(t, node_index, scale)
            owner = jnp.broadcast_to(e, (NODE, LANES))
            weights = jnp.concatenate(
                [jnp.where(owner == float(a), basis_r, 0.0) for a in range(elements)],
                axis=0,
            ).astype(jnp.bfloat16)
            tensor = [basis_s[j : j + 1] * basis_t for j in range(NODE)]
            partial = jnp.dot(
                fields_t[...], weights, preferred_element_type=jnp.float32
            )
            for c in range(field_count):
                base = c * NODE * NODE
                total = partial[base : base + NODE] * tensor[0]
                for j in range(1, NODE):
                    at = base + j * NODE
                    total += partial[at : at + NODE] * tensor[j]
                results.append(jnp.sum(total, axis=0, keepdims=True))
        result = jnp.concatenate(results, axis=0)
        back = jnp.transpose(result)
        back = jnp.concatenate(
            [back[k * width : (k + 1) * width] for k in range(packed)], axis=1
        )
        for h in range(back.shape[1] // LANES):
            send_value[h, rows] = back[:, h * LANES : (h + 1) * LANES]

    if n <= LANES:
        evaluate(0)
    else:
        lax.fori_loop(0, n // width, lambda b, c: (evaluate(b), c)[1], 0)

    exchange(send_value, recv_value, sems.at[3], sems.at[4], sems.at[5])

    cells = field_count * slots
    row = lax.broadcasted_iota(jnp.int32, (cells, cells), 0)
    lane = lax.broadcasted_iota(jnp.int32, (cells, cells), 1)
    source = (row % slots) * field_count + row // slots
    order = (lane == source).astype(jnp.float32).astype(jnp.bfloat16)

    finish(send_value, recv_value, sems.at[4], sems.at[5])

    gathered = jnp.concatenate(
        [recv_value[h] for h in range(cells // LANES)], axis=1
    ).astype(jnp.bfloat16)
    values = lax.dot_general(
        order, gathered, (((1,), (1,)), ((), ())), preferred_element_type=jnp.float32
    )
    out_ref[...] = values.astype(jnp.bfloat16).reshape(field_count, slots, n)
    rest = pl.ds(0, n - 1)
    for buffer, other, sem in (
        (send_query, recv_query, sems.at[0]),
        (send_value, recv_value, sems.at[3]),
    ):
        pltpu.make_async_copy(buffer.at[:, rest], other.at[:, rest], sem).wait()


def solution(mesh):
    def on_device(query_coords, owner_element, pair_counts, fields):
        wide_size, narrow_size = mesh.shape["wide"], mesh.shape["narrow"]
        n = wide_size * narrow_size
        slots = owner_element.shape[1]
        elements, node, columns = fields.shape
        field_count = columns // (node * node)
        cells = field_count * slots
        sizes = (wide_size, narrow_size, slots, elements, field_count)
        values = pl.pallas_call(
            functools.partial(kernel, sizes),
            out_shape=jax.ShapeDtypeStruct((field_count, slots, n), jnp.bfloat16),
            in_specs=[pl.BlockSpec(memory_space=pl.ANY)] * 4,
            out_specs=pl.BlockSpec(memory_space=pltpu.VMEM),
            scratch_shapes=[
                pltpu.VMEM((3, slots, n), jnp.float32),
                pltpu.VMEM((slots, n), jnp.int32),
                pltpu.VMEM((1, n), jnp.int32),
                pltpu.VMEM(fields.shape, jnp.bfloat16),
                pltpu.VMEM((columns, elements * node), jnp.bfloat16),
                pltpu.VMEM((1, n, LANES), jnp.float32),
                pltpu.VMEM((1, n, LANES), jnp.float32),
                pltpu.VMEM((cells // LANES, n, LANES), jnp.float32),
                pltpu.VMEM((cells // LANES, n, LANES), jnp.float32),
                pltpu.SemaphoreType.DMA((4,)),
                pltpu.SemaphoreType.DMA((6,)),
            ],
            compiler_params=pltpu.CompilerParams(
                collective_id=0, has_side_effects=True
            ),
            name="exchange_and_evaluate",
        )(query_coords[:, 0], owner_element[0], pair_counts, fields)
        return values[:, None]

    placed = (
        P(None, ("wide", "narrow"), None, None),
        P(("wide", "narrow"), None, None),
        P(("wide", "narrow"), None),
        P(("wide", "narrow"), None, None),
    )
    return jax.shard_map(
        on_device,
        mesh=mesh,
        in_specs=placed,
        out_specs=P(None, ("wide", "narrow"), None, None),
        check_vma=False,
    )
```

time: 51.9 us -> 19.8 us (0.38)
  blocking collectives: 35.3 us -> 0 us
  Pallas kernels: 0 us -> 18.1 us
  local copies, waits for them, and re-layouts: 13.2 us -> 1.47 us
  other arithmetic: 2.05 us -> 0 us
  matrix products: 0.69 us -> 0 us
    all_to_all x4 -> x0, blocking collectives: 35.3 us -> none  [the longest x1 13.7 us: on_device(): lax.all_to_all(payload, 'wide', split_axis=2, concat_axis=2, tiled=True)]
    pallas_call x0 -> x1, Pallas kernels: none -> 18.1 us  [on_device(): pl.pallas_call(functools.partial(kernel, sizes), out_shape=jax.ShapeDtype...]
    mul x32 -> x0, local copies, waits for them, and re-layouts: 5.1 us -> none  [lagrange(): factor * ((position - GLL_NODES[m]) / (GLL_NODES[i] - GLL_NODES[m]))]
    another operation x21 -> x0, local copies, waits for them, and re-layouts: 3.21 us -> none
    unnamed x16 -> x1, local copies, waits for them, and re-layouts: 3.02 us -> 1.47 us
    all_to_all x2 -> x0, other arithmetic: 1.34 us -> none  [the longest x1 0.67 us: on_device(): lax.all_to_all(lax.all_to_all(payload, 'wide', split_axis=2, concat_axis=...]
    reshape x1 -> x0, local copies, waits for them, and re-layouts: 0.8 us -> none  [on_device(): return returned.reshape(returned.shape[0], 1, slot_count, device_count)]
    all_to_all x4 -> x0, local copies, waits for them, and re-layouts: 0.77 us -> none  [the longest x2 0.53 us: on_device(): lax.all_to_all(payload, 'wide', split_axis=2, concat_axis=2, tiled=True)]
where the time goes in v1:
time: 19.8 us; the launch traced here: 19.6 us
  Pallas kernels  18.1 us (91%)
  local copies, waits for them, and re-layouts  1.47 us (7%)
    pallas_call x1, Pallas kernels, on_device(): pl.pallas_call(functools.partial(kernel, sizes), out_shape=jax.ShapeDtype...  18.1 us
    unnamed x1, local copies, waits for them, and re-layouts  1.47 us

profile of v1, /device:TPU:0, one launch (start us, length us, event | category | flops | bytes accessed | tf_op | source)
XLA Modules:
  0.0 19.6 jit_solution(3758005230427562760)
XLA Ops:
  0.0 18.1 %exchange_and_evaluate.1 = bf16[16,16,32]{2,1,0:T(8,128)(2,1)} custom-call(f32[3,16,32]{2,1,0:T(8,128)} %bitcast.6, s32[16,32]{1,0:T(8,128)} %bitcast.7, s32[1,32]{1,0:T(1,128)} %counts_hbm.1, bf16[16,8,1024]{2,1,0:T(8,128)(2,1)} %fields_hbm.1), custom_call_target="tpu_custom_call" | custom-call | tf_op jit(solution)/shard_map/exchange_and_evaluate/pallas_call | solution.py:242
  18.1 1.5 %copy.7 = bf16[16,1,16,32]{3,2,1,0:T(8,128)(2,1)} copy(bf16[16,1,16,32]{3,2,1,0:T(8,128)(2,1)} %bitcast.5) | data formatting | bytes 32768

commit v2 on v1

--- a/solution.py
+++ b/solution.py
@@ -43,7 +43,7 @@
     element_hbm,
     counts_hbm,
     fields_hbm,
-    out_ref,
+    recv_value,
     coords,
     element,
     counts,
@@ -52,7 +52,6 @@
     send_query,
     recv_query,
     send_value,
-    recv_value,
     local_sems,
     sems,
 ):
@@ -63,7 +62,26 @@
     groups = slots // packed
     me = lax.axis_index("wide") * narrow_size + lax.axis_index("narrow")
 
+    def flipped(value, size):
+        options = [value]
+        bit = 1
+        while bit < size:
+            turn = bit * (1 - 2 * (value // bit % 2))
+            options += [option + turn for option in options]
+            bit *= 2
+        return options
+
+    mirrored = n <= 64 and n & (n - 1) == 0
+    if mirrored:
+        wide_options = flipped(lax.axis_index("wide"), wide_size)
+        narrow_options = flipped(lax.axis_index("narrow"), narrow_size)
+
     def partner(step):
+        if mirrored:
+            mask = n - 1 - step
+            wide = wide_options[mask // narrow_size]
+            narrow = narrow_options[mask % narrow_size]
+            return wide * narrow_size + narrow, (wide, narrow)
         offset = n // 2 + (1 - 2 * (step % 2)) * ((step + 1) // 2)
         index = lax.rem(me + offset, n)
         return index, (index // narrow_size, lax.rem(index, narrow_size))
@@ -207,27 +225,34 @@
 
     exchange(send_value, recv_value, sems.at[3], sems.at[4], sems.at[5])
 
-    cells = field_count * slots
-    row = lax.broadcasted_iota(jnp.int32, (cells, cells), 0)
-    lane = lax.broadcasted_iota(jnp.int32, (cells, cells), 1)
-    source = (row % slots) * field_count + row // slots
-    order = (lane == source).astype(jnp.float32).astype(jnp.bfloat16)
-
     finish(send_value, recv_value, sems.at[4], sems.at[5])
 
-    gathered = jnp.concatenate(
-        [recv_value[h] for h in range(cells // LANES)], axis=1
-    ).astype(jnp.bfloat16)
-    values = lax.dot_general(
-        order, gathered, (((1,), (1,)), ((), ())), preferred_element_type=jnp.float32
-    )
-    out_ref[...] = values.astype(jnp.bfloat16).reshape(field_count, slots, n)
     rest = pl.ds(0, n - 1)
     for buffer, other, sem in (
         (send_query, recv_query, sems.at[0]),
         (send_value, recv_value, sems.at[3]),
     ):
         pltpu.make_async_copy(buffer.at[:, rest], other.at[:, rest], sem).wait()
+
+
+def unpack(sizes, received, out_ref, recv_value, sem):
+    field_count, slots, n = sizes
+    load = pltpu.make_async_copy(received, recv_value, sem)
+    load.start()
+    cells = field_count * slots
+    row = lax.broadcasted_iota(jnp.int32, (cells, cells), 0)
+    lane = lax.broadcasted_iota(jnp.int32, (cells, cells), 1)
+    source = (row % slots) * field_count + row // slots
+    order = (lane == source).astype(jnp.float32).astype(jnp.bfloat16)
+
+    load.wait()
+    gathered = jnp.concatenate(
+        [recv_value[h] for h in range(cells // LANES)], axis=1
+    ).astype(jnp.bfloat16)
+    values = lax.dot_general(
+        order, gathered, (((1,), (1,)), ((), ())), preferred_element_type=jnp.float32
+    )
+    out_ref[...] = values.astype(jnp.bfloat16).reshape(field_count, slots, n)
 
 
 def solution(mesh):
@@ -239,11 +264,11 @@
         field_count = columns // (node * node)
         cells = field_count * slots
         sizes = (wide_size, narrow_size, slots, elements, field_count)
-        values = pl.pallas_call(
+        received = pl.pallas_call(
             functools.partial(kernel, sizes),
-            out_shape=jax.ShapeDtypeStruct((field_count, slots, n), jnp.bfloat16),
+            out_shape=jax.ShapeDtypeStruct((cells // LANES, n, LANES), jnp.float32),
             in_specs=[pl.BlockSpec(memory_space=pl.ANY)] * 4,
-            out_specs=pl.BlockSpec(memory_space=pltpu.VMEM),
+            out_specs=pl.BlockSpec(memory_space=pl.ANY),
             scratch_shapes=[
                 pltpu.VMEM((3, slots, n), jnp.float32),
                 pltpu.VMEM((slots, n), jnp.int32),
@@ -253,7 +278,6 @@
                 pltpu.VMEM((1, n, LANES), jnp.float32),
                 pltpu.VMEM((1, n, LANES), jnp.float32),
                 pltpu.VMEM((cells // LANES, n, LANES), jnp.float32),
-                pltpu.VMEM((cells // LANES, n, LANES), jnp.float32),
                 pltpu.SemaphoreType.DMA((4,)),
                 pltpu.SemaphoreType.DMA((6,)),
             ],
@@ -262,6 +286,17 @@
             ),
             name="exchange_and_evaluate",
         )(query_coords[:, 0], owner_element[0], pair_counts, fields)
+        values = pl.pallas_call(
+            functools.partial(unpack, (field_count, slots, n)),
+            out_shape=jax.ShapeDtypeStruct((field_count, slots, n), jnp.bfloat16),
+            in_specs=[pl.BlockSpec(memory_space=pl.ANY)],
+            out_specs=pl.BlockSpec(memory_space=pltpu.VMEM),
+            scratch_shapes=[
+                pltpu.VMEM(received.shape, received.dtype),
+                pltpu.SemaphoreType.DMA,
+            ],
+            name="unpack",
+        )(received)
         return values[:, None]
 
     placed = (

time: 19.8 us -> 18.4 us (0.929)
  local copies, waits for them, and re-layouts: 1.47 us -> 0 us
    pallas_call x0 -> x1, Pallas kernels: none -> 1.56 us  [on_device(): pl.pallas_call(functools.partial(unpack, (field_count, slots, n)), out_sh...]
    unnamed x1 -> x0, local copies, waits for them, and re-layouts: 1.47 us -> none
    pallas_call x1, Pallas kernels: 18.1 us -> 16.7 us  [on_device(): pl.pallas_call(functools.partial(kernel, sizes), out_shape=jax.ShapeDtype...]
where the time goes in v2:
time: 18.4 us; the launch traced here: 18.3 us
  Pallas kernels  18.2 us (99%)
    pallas_call x1, Pallas kernels, on_device(): pl.pallas_call(functools.partial(kernel, sizes), out_shape=jax.ShapeDtype...  16.7 us
    pallas_call x1, Pallas kernels, on_device(): pl.pallas_call(functools.partial(unpack, (field_count, slots, n)), out_sh...  1.56 us

profile of v2, /device:TPU:0, one launch (start us, length us, event | category | flops | bytes accessed | tf_op | source)
XLA Modules:
  0.0 18.3 jit_solution(12535664172990048038)
XLA Ops:
  0.0 16.7 %exchange_and_evaluate.1.received = f32[2,32,128]{2,1,0:T(8,128)} custom-call(f32[3,16,32]{2,1,0:T(8,128)} %bitcast.5, s32[16,32]{1,0:T(8,128)} %bitcast.6, s32[1,32]{1,0:T(1,128)} %counts_hbm.1, bf16[16,8,1024]{2,1,0:T(8,128)(2,1)} %fields_hbm.1), custom_call_target="tpu_custom_call" | custom-call | tf_op jit(solution)/shard_map/exchange_and_evaluate/pallas_call | solution.py:267
  16.7 1.6 %unpack.1 = bf16[16,16,32]{2,1,0:T(8,128)(2,1)} custom-call(f32[2,32,128]{2,1,0:T(8,128)} %exchange_and_evaluate.1.received), custom_call_target="tpu_custom_call" | custom-call | tf_op jit(solution)/shard_map/unpack/pallas_call | solution.py:289
